TPU v7x, 32 devices: a whole 2x2x4 slice. The times are simulated.
32 devices in a mesh: ao: 8 (over y, x, core), aux: 4 (over z).
Axes of the slice: x: 2, y: 2, z: 4, core: 2. Of those that a mesh axis runs over, the one named last changes fastest.
Arguments:
- blocks: bfloat16 [48, 256, 128, 128], P('ao', 'aux'), may hold values from -6 to 6
- pairs: int32 [48, 2], P('ao'), may hold values from 0 to 79, as said below
- counts: int32 [8], P('ao'), may hold values from 1 to 6, as said below
- owned_blocks: int32 [80], P('ao'), may hold values from 0 to 79, as said below
- occ_coef: bfloat16 [80, 8, 128], P('ao'), may hold values from -0.5 to 0.5
- vir_coef: bfloat16 [10240, 9216], P('ao', 'aux'), may hold values from -0.109375 to 0.109375
Outputs:
- b_tensor: bfloat16 [256, 8, 9216], P('ao', None, 'aux')
Inputs may be any that keep to these rules, and one draw needn't show every extreme that they name: `pairs`: among the used slots of one ao index, at most 3 have nu blocks whose rows one owner holds; in every draw some index reaches 3. `counts`: some ao index uses all 6 slots in every draw. `owned_blocks`: every atom block appears exactly once.
All inputs are finite; a program needn't handle non-finite values.
Results may differ from a plain program's by a relative error of at most 0.014.
Values may be sent and summed in bfloat16 or wider, within the bound.
A program may use at most 128 MiB of HBM per device.

v0:
```python
import jax
import jax.numpy as jnp
from jax import lax
from jax.sharding import PartitionSpec as P


def block_place(block_ids, owned_all):
    hits = block_ids[..., None] == owned_all
    positions = jnp.arange(owned_all.shape[0], dtype=jnp.int32)
    return jnp.sum(jnp.where(hits, positions, 0), axis=-1)


def per_device(blocks, pairs, counts, owned_blocks, occ_coef, vir_coef):
    groups = lax.axis_size("ao")
    own_index = lax.axis_index("ao")
    slot_count = blocks.shape[0]
    aux_depth = blocks.shape[1]
    block_width = blocks.shape[3]
    occupied = occ_coef.shape[1]
    all_pairs, all_counts, all_owned = (
        lax.all_gather(pairs, "ao", axis=0, tiled=True),
        lax.all_gather(counts, "ao", axis=0, tiled=True),
        lax.all_gather(owned_blocks, "ao", axis=0, tiled=True),
    )
    occ_all = lax.all_gather(occ_coef, "ao", axis=0, tiled=True)
    total_blocks = all_owned.shape[0]
    per_owner = total_blocks // groups
    slot_ids = jnp.arange(slot_count, dtype=jnp.int32)
    in_use = slot_ids < counts[0]
    occ_pick = occ_all[block_place(pairs[:, 0], all_owned)]
    slab_values = jnp.einsum("sim,spmn->spin", occ_pick, blocks, preferred_element_type=jnp.float32)
    slab_values = jnp.where(in_use[:, None, None, None], slab_values, 0.0).astype(jnp.bfloat16)
    flat_slabs = slab_values.reshape(slot_count, aux_depth * occupied, block_width)
    place_all = block_place(all_pairs[:, 1], all_owned).reshape(groups, slot_count)
    owner_all = place_all // per_owner
    local_all = place_all % per_owner
    live_all = slot_ids[None, :] < all_counts[:, None]
    mine_all = live_all & (owner_all == own_index)
    local_ids = jnp.arange(per_owner, dtype=jnp.int32)
    slabs_got = lax.all_gather(flat_slabs, "ao", axis=0, tiled=True)
    assign = (
        mine_all.reshape(-1)[None, :] & (local_all.reshape(-1)[None, :] == local_ids[:, None])
    ).astype(jnp.bfloat16)
    summed = jnp.einsum("lt,tqm->qlm", assign, slabs_got, preferred_element_type=jnp.float32)
    rows_local = summed.reshape(summed.shape[0], per_owner * block_width).astype(jnp.bfloat16)
    rows_whole = lax.all_gather(rows_local, "aux", axis=0, tiled=True)
    share = rows_whole.shape[0] // groups
    result = lax.psum_scatter(
        jnp.dot(rows_whole, vir_coef, preferred_element_type=jnp.float32).astype(jnp.bfloat16),
        "ao",
        scatter_dimension=0,
        tiled=True,
    ).astype(jnp.float32)
    return result.reshape(share // occupied, occupied, vir_coef.shape[1]).astype(jnp.bfloat16)


def solution(mesh):
    in_specs = (
        P("ao", "aux", None, None),
        P("ao", None),
        P("ao"),
        P("ao"),
        P("ao", None, None),
        P("ao", "aux"),
    )
    out_specs = P("ao", None, "aux")
    return jax.shard_map(
        per_device, mesh=mesh, in_specs=in_specs, out_specs=out_specs, check_vma=False
    )
```

profile of v0, /device:TPU:0, one launch (start us, length us, event | category | flops | bytes accessed | tf_op | source)
XLA Modules:
  0.0 291.0 jit_solution(9892513670469097050)
XLA Ops:
  6.5 0.0 all-gather.4.cloned.1.call-start
  7.2 0.7 slice_bitcast_fusion.1
  7.9 1.3 dynamic-slice
  9.9 0.8 dynamic-update-slice.1
  10.7 0.8 dynamic-update-slice
  11.5 9.5 %all-reduce.2 = (s32[80]{0:T(128)S(1)}, s32[8]{0:T(128)S(1)}) all-reduce(s32[80]{0:T(128)S(1)} %dynamic-update-slice, s32[8]{0:T(128)S(1)} %dynamic-update-slice.1), channel_id=1, replica_groups=mesh['ao'=8,'aux'=4] {'ao'}, use_global_device_ids=true, to_apply=%add | all-reduce | flops 88 | bytes 704
  21.0 0.2 select_reduce_fusion.1
  21.2 8.6 %all_gather.18 = bf16[80,8,128]{2,1,0:T(8,128)(2,1)S(1)} all-gather(bf16[10,8,128]{2,1,0:T(8,128)(2,1)} %param.10), channel_id=1, replica_groups=mesh['ao'=8,'aux'=4] {'ao'}, dimensions={0}, use_global_device_ids=true | all-gather | bytes 184320 | tf_op jit(solution)/shard_map/all_gather | solution.py:25
  29.8 0.6 gather_fusion
  30.4 0.0 copy-start
  30.4 7.2 %fusion.4 = bf16[6,512,128]{2,1,0:T(8,128)(2,1)} fusion(bf16[6,64,128,128]{3,2,1,0:T(8,128)(2,1)} %param.6, pred[6]{0:T(512)(128)(4,1)S(1)} %iota_compare_fusion.2, bf16[6,8,128]{2,1,0:T(8,128)(2,1)S(1)} %gather_fusion), kind=kOutput, calls=%fused_computation.6 | convolution fusion | flops 101449728 | bytes 13381638 | tf_op jit(solution)/shard_map/sim,spmn->spin/dot_general | solution.py:31
  37.6 0.0 all-gather.4.cloned.1.call-update
  37.6 0.0 all-gather.6.cloned.1.call-start
  37.7 0.1 iota_compare_fusion.1
  37.8 0.1 lt.52
  37.9 0.0 copy-done
  37.9 8.6 %all-gather = s32[8,6,2]{1,2,0:T(2,128)S(1)} all-gather(s32[1,6,2]{1,2,0:T(2,128)S(1)} %bitcast.35), channel_id=1, replica_groups=mesh['ao'=8,'aux'=4] {'ao'}, dimensions={0}, use_global_device_ids=true | all-gather | bytes 432 | tf_op jit(solution)/shard_map/all_gather | solution.py:21
  46.5 0.1 reshape.75
  46.5 0.2 select_reduce_fusion
  46.8 36.7 %all-gather.4.cloned.1.call-done = bf16[48,512,128]{2,1,0:T(8,128)(2,1)} async-done(((bf16[6,512,128]{2,1,0:T(8,128)(2,1)}), bf16[48,512,128]{2,1,0:T(8,128)(2,1)}) %all-gather.4.cloned.1.call-update) | async-done | bytes 6291472 | tf_op jit(solution)/shard_map/all_gather | solution.py:40
  83.5 6.4 %convert_bitcast_fusion = bf16[512,10,128]{2,1,0:T(8,128)(2,1)S(1)} fusion(bf16[48,512,128]{2,1,0:T(8,128)(2,1)} %all-gather.4.cloned.1.call-done, s32[48]{0:T(128)S(1)} %and_select_fusion, pred[48]{0:T(512)(128)(4,1)S(1)} %compare_and_fusion), kind=kOutput, calls=%fused_computation.4 | convolution fusion | flops 63570880 | bytes 7602416 | tf_op jit(solution)/shard_map/lt,tqm->qlm/dot_general | solution.py:44
  89.9 2.6 copy.17
  92.5 0.0 all-gather.6.cloned.1.call-update
  92.5 0.2 reduce-scatter.2.cloned.1.call-start
  92.7 98.0 %all-gather.6.cloned.1.call-done = bf16[2048,1280]{0,1:T(8,128)(2,1)} async-done(((bf16[512,1280]{0,1:T(8,128)(2,1)}), bf16[2048,1280]{0,1:T(8,128)(2,1)}) %all-gather.6.cloned.1.call-update) | async-done | bytes 5242896 | tf_op jit(solution)/shard_map/all_gather | solution.py:46
  190.7 18.4 %convolution_convert_fusion = bf16[2048,2304]{1,0:T(8,128)(2,1)} fusion(bf16[2048,1280]{0,1:T(8,128)(2,1)} %all-gather.6.cloned.1.call-done, bf16[1280,2304]{1,0:T(8,128)(2,1)} %param.11), kind=kOutput, calls=%fused_computation.1 | convolution fusion | flops 12084314112 | bytes 20578304 | tf_op jit(solution)/shard_map/dot_general | solution.py:49
  209.1 0.0 reduce-scatter.2.cloned.1.call-update
  209.1 75.3 %reduce-scatter.2.cloned.1.call-done = bf16[256,2304]{1,0:T(8,128)(2,1)} async-done(((bf16[2048,2304]{1,0:T(8,128)(2,1)}), bf16[256,2304]{1,0:T(8,128)(2,1)}) %reduce-scatter.2.cloned.1.call-update) | async-done | bytes 1179664 | tf_op jit(solution)/shard_map/reduce_scatter | solution.py:48
  (9 shorter events, 0.1 us)
Async XLA Ops:
  6.5 76.9 %all-gather.4.cloned.1.call-start = ((), (), s32[]{:S(2)}) async-start(), calls=%async_computation.1 | async-start | bytes 7077888 | tf_op jit(solution)/shard_map/all_gather | solution.py:40
  30.4 7.5 %copy-start = (s32[6,2]{0,1:T(2,128)S(1)}, s32[6,2]{0,1:T(2,128)}, u32[]{:S(2)}) copy-start(s32[6,2]{0,1:T(2,128)} %param.7) | copy-start | bytes 148
  37.6 153.0 %all-gather.6.cloned.1.call-start = ((), (), s32[]{:S(2)}) async-start(), calls=%async_computation.2 | async-start | bytes 6553600 | tf_op jit(solution)/shard_map/all_gather | solution.py:46
  92.5 191.9 %reduce-scatter.2.cloned.1.call-start = ((), (), s32[]{:S(2)}) async-start(), calls=%async_computation.3 | async-start | bytes 10616832 | tf_op jit(solution)/shard_map/reduce_scatter | solution.py:48
Sparse Core Ops, SparseCore 0:
  37.8 45.6 all-gather.3
  92.6 98.0 all-gather.5
  209.2 75.1 reduce-scatter.1
where the time goes:
time: 291 us
  waiting for transfers between devices  210 us (72%)
  matrix products  32.1 us (11%)
  blocking collectives  26.7 us (9%)
  between operations  14.5 us (5%)
  local copies, waits for them, and re-layouts  6.95 us (2%)
    all_gather x1, waiting for transfers between devices, per_device(): rows_whole = lax.all_gather(rows_local, 'aux', axis=0, tiled=True)  98 us
    reduce_scatter x1, waiting for transfers between devices, per_device(): lax.psum_scatter(jnp.dot(rows_whole, vir_coef, preferred_element_type=jnp...  75.3 us
    all_gather x1, waiting for transfers between devices, per_device(): slabs_got = lax.all_gather(flat_slabs, 'ao', axis=0, tiled=True)  36.7 us
    dot_general x1, matrix products, per_device(): jnp.dot(rows_whole, vir_coef, preferred_element_type=jnp.float32)  18.4 us
    unnamed x1, blocking collectives  9.49 us
    all_gather x1, blocking collectives, per_device(): occ_all = lax.all_gather(occ_coef, 'ao', axis=0, tiled=True)  8.6 us
    all_gather x1, blocking collectives, per_device(): lax.all_gather(pairs, 'ao', axis=0, tiled=True)  8.59 us
    dot_general x1, matrix products, per_device(): jnp.einsum('sim,spmn->spin', occ_pick, blocks, preferred_element_type=jnp...  7.2 us
  transfers between devices with their start and end apart: 3, of which 3 were waited for; matrix products, arithmetic and copies ran while one was open for 0% of the time, Pallas kernels for 0%

commit v1 on v0

--- a/solution.py
+++ b/solution.py
@@ -37,11 +37,41 @@
     live_all = slot_ids[None, :] < all_counts[:, None]
     mine_all = live_all & (owner_all == own_index)
     local_ids = jnp.arange(per_owner, dtype=jnp.int32)
-    slabs_got = lax.all_gather(flat_slabs, "ao", axis=0, tiled=True)
     assign = (
         mine_all.reshape(-1)[None, :] & (local_all.reshape(-1)[None, :] == local_ids[:, None])
     ).astype(jnp.bfloat16)
-    summed = jnp.einsum("lt,tqm->qlm", assign, slabs_got, preferred_element_type=jnp.float32)
+    size, index, rows = (lax.axis_size("ao"), lax.axis_index("ao"), flat_slabs.shape[0])
+    right = [(i, (i + 1) % size) for i in range(size)]
+    left = [(i, (i - 1) % size) for i in range(size)]
+    middle = size // 2
+    from_left = from_right = flat_slabs
+    total = jnp.einsum(
+        "lt,tqm->qlm",
+        lax.dynamic_slice_in_dim(assign, index * rows, flat_slabs.shape[0], axis=1),
+        flat_slabs,
+        preferred_element_type=jnp.float32,
+    )
+    for step in range(1, middle + 1):
+        from_left = lax.ppermute(from_left, "ao", right)
+        if step < size - middle:
+            from_right = lax.ppermute(from_right, "ao", left)
+            total = total + jnp.einsum(
+                "lt,tqm->qlm",
+                lax.dynamic_slice_in_dim(
+                    assign, (index + step) % size * rows, from_right.shape[0], axis=1
+                ),
+                from_right,
+                preferred_element_type=jnp.float32,
+            )
+        total = total + jnp.einsum(
+            "lt,tqm->qlm",
+            lax.dynamic_slice_in_dim(
+                assign, (index - step) % size * rows, from_left.shape[0], axis=1
+            ),
+            from_left,
+            preferred_element_type=jnp.float32,
+        )
+    summed = total
     rows_local = summed.reshape(summed.shape[0], per_owner * block_width).astype(jnp.bfloat16)
     rows_whole = lax.all_gather(rows_local, "aux", axis=0, tiled=True)
     share = rows_whole.shape[0] // groups

time: 291 us -> 322 us (1.11)
  matrix products: 32.1 us -> 48.1 us
  blocking collectives: 26.7 us -> 37.7 us
  starting transfers between devices: 0.27 us -> 8.35 us
  waiting for transfers between devices: 210 us -> 204 us
    all_gather x1 -> x0, waiting for transfers between devices: 36.7 us -> none  [per_device(): slabs_got = lax.all_gather(flat_slabs, 'ao', axis=0, tiled=True)]
    ppermute x0 -> x7, waiting for transfers between devices: none -> 31.2 us  [the longest x4 31.2 us: per_device(): from_left = lax.ppermute(from_left, 'ao', right)]
    dot_general x1 -> x8, matrix products: 6.43 us -> 23.4 us  [the longest x4 15.3 us: per_device(): jnp.einsum('lt,tqm->qlm', lax.dynamic_slice_in_dim(assign, (index - step)...]
    all_gather x1, blocking collectives: 8.59 us -> 19.6 us  [per_device(): lax.all_gather(pairs, 'ao', axis=0, tiled=True)]
    ppermute x0 -> x7, starting transfers between devices: none -> 8.12 us  [the longest x3 7.34 us: per_device(): from_right = lax.ppermute(from_right, 'ao', left)]
  transfers between devices with their start and end apart: 3 -> 9, of which waited for: 3 -> 5; matrix products, arithmetic and copies ran while one was open for 0% -> 5% of each run, Pallas kernels for 0% -> 0%
where the time goes in v1:
time: 322 us
  waiting for transfers between devices  204 us (63%)
  matrix products  48.1 us (15%)
  blocking collectives  37.7 us (12%)
  between operations  14.8 us (5%)
  local copies, waits for them, and re-layouts  8.45 us (3%)
  starting transfers between devices  8.35 us (3%)
    all_gather x1, waiting for transfers between devices, per_device(): rows_whole = lax.all_gather(rows_local, 'aux', axis=0, tiled=True)  97.3 us
    reduce_scatter x1, waiting for transfers between devices, per_device(): lax.psum_scatter(jnp.dot(rows_whole, vir_coef, preferred_element_type=jnp...  75.3 us
    ppermute x4, waiting for transfers between devices, per_device(): from_left = lax.ppermute(from_left, 'ao', right)  31.2 us
    all_gather x1, blocking collectives, per_device(): lax.all_gather(pairs, 'ao', axis=0, tiled=True)  19.6 us
    dot_general x1, matrix products, per_device(): jnp.dot(rows_whole, vir_coef, preferred_element_type=jnp.float32)  18.4 us
    dot_general x4, matrix products, per_device(): jnp.einsum('lt,tqm->qlm', lax.dynamic_slice_in_dim(assign, (index - step)...  15.3 us
    unnamed x1, blocking collectives  9.49 us
    all_gather x1, blocking collectives, per_device(): occ_all = lax.all_gather(occ_coef, 'ao', axis=0, tiled=True)  8.6 us
  transfers between devices with their start and end apart: 9, of which 5 were waited for; matrix products, arithmetic and copies ran while one was open for 5% of the time, Pallas kernels for 0%

profile of v1, /device:TPU:0, one launch (start us, length us, event | category | flops | bytes accessed | tf_op | source)
XLA Modules:
  0.0 321.8 jit_solution(14239300980116273984)
XLA Ops:
  6.5 0.0 all-gather.3.cloned.1.call-start
  7.2 0.7 slice_bitcast_fusion.1
  7.9 1.2 dynamic-slice
  9.8 0.7 dynamic-update-slice.1
  10.5 0.8 dynamic-update-slice
  11.3 9.5 %all-reduce.2 = (s32[80]{0:T(128)S(1)}, s32[8]{0:T(128)S(1)}) all-reduce(s32[80]{0:T(128)S(1)} %dynamic-update-slice, s32[8]{0:T(128)S(1)} %dynamic-update-slice.1), channel_id=1, replica_groups=mesh['ao'=8,'aux'=4] {'ao'}, use_global_device_ids=true, to_apply=%add | all-reduce | flops 88 | bytes 704
  20.8 0.2 select_reduce_fusion.1
  21.0 8.6 %all_gather.15 = bf16[80,8,128]{2,1,0:T(8,128)(2,1)S(1)} all-gather(bf16[10,8,128]{2,1,0:T(8,128)(2,1)} %param.10), channel_id=1, replica_groups=mesh['ao'=8,'aux'=4] {'ao'}, dimensions={0}, use_global_device_ids=true | all-gather | bytes 184320 | tf_op jit(solution)/shard_map/all_gather | solution.py:25
  29.6 0.6 gather_fusion
  30.2 0.0 copy-start.1
  30.2 6.3 %fusion.1 = bf16[6,512,128]{2,1,0:T(8,128)(2,1)S(1)} fusion(bf16[6,64,128,128]{3,2,1,0:T(8,128)(2,1)} %param.6, pred[6]{0:T(512)(128)(4,1)S(1)} %iota_compare_fusion.2, bf16[6,8,128]{2,1,0:T(8,128)(2,1)S(1)} %gather_fusion), kind=kOutput, calls=%fused_computation.5 | convolution fusion | flops 101449728 | bytes 13381638 | tf_op jit(solution)/shard_map/sim,spmn->spin/dot_general | solution.py:31
  36.5 0.4 collective-permute-start.1
  36.9 2.3 collective-permute-start
  39.2 0.0 copy-done.1
  39.2 19.6 %all-gather = s32[8,6,2]{1,2,0:T(2,128)S(1)} all-gather(s32[1,6,2]{1,2,0:T(2,128)S(1)} %bitcast.56), channel_id=1, replica_groups=mesh['ao'=8,'aux'=4] {'ao'}, dimensions={0}, use_global_device_ids=true | all-gather | bytes 432 | tf_op jit(solution)/shard_map/all_gather | solution.py:21
  58.8 0.1 reshape.75
  58.9 0.1 iota_compare_fusion.1
  59.0 0.1 lt.106
  59.1 0.2 select_reduce_fusion
  59.3 0.0 collective-permute-done.1
  59.3 0.4 collective-permute-start.3
  59.7 0.1 fusion.17
  59.8 0.0 collective-permute-done
  59.8 2.4 collective-permute-start.2
  62.1 2.7 fusion.15
  64.8 13.9 %collective-permute-done.3 = bf16[6,512,128]{2,1,0:T(8,128)(2,1)S(1)} collective-permute-done((bf16[6,512,128]{2,1,0:T(8,128)(2,1)S(1)}, bf16[6,512,128]{2,1,0:T(8,128)(2,1)S(1)}, u32[]{:S(2)}, u32[]{:S(2)}) %collective-permute-start.3) | collective-permute-done | bytes 786464 | tf_op jit(solution)/shard_map/ppermute | solution.py:55
  78.7 0.0 collective-permute-start.5
  78.7 0.8 fusion.13
  79.5 0.8 fusion.11
  80.3 0.0 collective-permute-done.2
  80.3 2.7 collective-permute-start.4
  83.0 1.9 fusion.9
  84.9 13.0 %collective-permute-done.5 = bf16[6,512,128]{2,1,0:T(8,128)(2,1)S(1)} collective-permute-done((bf16[6,512,128]{2,1,0:T(8,128)(2,1)S(1)}, bf16[6,512,128]{2,1,0:T(8,128)(2,1)S(1)}, u32[]{:S(2)}, u32[]{:S(2)}) %collective-permute-start.5) | collective-permute-done | bytes 786464 | tf_op jit(solution)/shard_map/ppermute | solution.py:55
  97.9 0.0 collective-permute-start.6
  97.9 2.7 fusion.7
  100.7 0.0 copy-start
  100.7 2.7 fusion.3
  103.4 0.0 collective-permute-done.4
  103.4 2.7 fusion.5
  106.1 4.2 %collective-permute-done.6 = bf16[6,512,128]{2,1,0:T(8,128)(2,1)} collective-permute-done((bf16[6,512,128]{2,1,0:T(8,128)(2,1)S(1)}, bf16[6,512,128]{2,1,0:T(8,128)(2,1)}, u32[]{:S(2)}, u32[]{:S(2)}) %collective-permute-start.6) | collective-permute-done | bytes 786464 | tf_op jit(solution)/shard_map/ppermute | solution.py:55
  110.4 0.0 copy-done
  110.4 9.1 %fusion = bf16[512,10,128]{2,1,0:T(8,128)(2,1)} fusion(f32[512,128,10]{1,2,0:T(8,128)} %fusion.3, f32[512,128,10]{1,2,0:T(8,128)} %fusion.5, f32[512,128,10]{1,2,0:T(8,128)} %fusion.7, f32[512,128,10]{1,2,0:T(8,128)S(1)} %fusion.9, f32[512,128,10]{1,2,0:T(8,128)S(1)} %fusion.11, f32[512,128,10]{1,2,0:T(8,128)S(1)} %copy-done, ...), kind=kOutput, calls=%fused_computation.3 | convolution fusion | flops 13107200 | bytes 26739716 | tf_op jit(solution)/shard_map/lt,tqm->qlm/dot_general | solution.py:66
  119.4 4.2 %copy.35 = bf16[512,10,128]{0,2,1:T(8,128)(2,1)} copy(bf16[512,10,128]{2,1,0:T(8,128)(2,1)} %fusion) | data formatting | bytes 2621440 | tf_op jit(solution)/shard_map/convert_element_type | solution.py:75
  123.6 0.0 all-gather.3.cloned.1.call-update
  123.7 0.2 reduce-scatter.2.cloned.1.call-start
  123.9 97.3 %all-gather.3.cloned.1.call-done = bf16[2048,1280]{0,1:T(8,128)(2,1)} async-done(((bf16[512,1280]{0,1:T(8,128)(2,1)}), bf16[2048,1280]{0,1:T(8,128)(2,1)}) %all-gather.3.cloned.1.call-update) | async-done | bytes 5242896 | tf_op jit(solution)/shard_map/all_gather | solution.py:76
  221.2 18.4 %convolution_convert_fusion = bf16[2048,2304]{1,0:T(8,128)(2,1)} fusion(bf16[2048,1280]{0,1:T(8,128)(2,1)} %all-gather.3.cloned.1.call-done, bf16[1280,2304]{1,0:T(8,128)(2,1)} %param.11), kind=kOutput, calls=%fused_computation.1 | convolution fusion | flops 12084314112 | bytes 20578304 | tf_op jit(solution)/shard_map/dot_general | solution.py:79
  239.6 0.0 reduce-scatter.2.cloned.1.call-update
  239.7 75.3 %reduce-scatter.2.cloned.1.call-done = bf16[256,2304]{1,0:T(8,128)(2,1)} async-done(((bf16[2048,2304]{1,0:T(8,128)(2,1)}), bf16[256,2304]{1,0:T(8,128)(2,1)}) %reduce-scatter.2.cloned.1.call-update) | async-done | bytes 1179664 | tf_op jit(solution)/shard_map/reduce_scatter | solution.py:78
  (9 shorter events, 0.1 us)
Async XLA Ops:
  6.5 214.7 %all-gather.3.cloned.1.call-start = ((), (), s32[]{:S(2)}) async-start(), calls=%async_computation.1 | async-start | bytes 6553600 | tf_op jit(solution)/shard_map/all_gather | solution.py:76
  30.2 9.0 %copy-start.1 = (s32[6,2]{0,1:T(2,128)S(1)}, s32[6,2]{0,1:T(2,128)}, u32[]{:S(2)}) copy-start(s32[6,2]{0,1:T(2,128)} %param.7) | copy-start | bytes 148
  36.5 22.8 %collective-permute-start.1 = (bf16[6,512,128]{2,1,0:T(8,128)(2,1)S(1)}, bf16[6,512,128]{2,1,0:T(8,128)(2,1)S(1)}, u32[]{:S(2)}, u32[]{:S(2)}) collective-permute-start(bf16[6,512,128]{2,1,0:T(8,128)(2,1)S(1)} %fusion.1), channel_id=1, source_target_pairs={{0,4},{4,8},{8,12},{12,16},{16,20},{20,24},{24,28},{28,0},{1,5},{5... | collective-permute-start | bytes 2359304 | tf_op jit(solution)/shard_map/ppermute | solution.py:55
  36.9 22.9 %collective-permute-start = (bf16[6,512,128]{2,1,0:T(8,128)(2,1)S(1)}, bf16[6,512,128]{2,1,0:T(8,128)(2,1)S(1)}, u32[]{:S(2)}, u32[]{:S(2)}) collective-permute-start(bf16[6,512,128]{2,1,0:T(8,128)(2,1)S(1)} %fusion.1), channel_id=1, source_target_pairs={{0,28},{4,0},{8,4},{12,8},{16,12},{20,16},{24,20},{28,24},{1,29},{... | collective-permute-start | bytes 2359304 | tf_op jit(solution)/shard_map/ppermute | solution.py:57
  59.3 19.5 %collective-permute-start.3 = (bf16[6,512,128]{2,1,0:T(8,128)(2,1)S(1)}, bf16[6,512,128]{2,1,0:T(8,128)(2,1)S(1)}, u32[]{:S(2)}, u32[]{:S(2)}) collective-permute-start(bf16[6,512,128]{2,1,0:T(8,128)(2,1)S(1)} %collective-permute-done.1), channel_id=1, source_target_pairs={{0,4},{4,8},{8,12},{12,16},{16,20},{20,24},{24,28},{28,0},{1,5},{5... | collective-permute-start | bytes 2359304 | tf_op jit(solution)/shard_map/ppermute | solution.py:55
  59.8 20.5 %collective-permute-start.2 = (bf16[6,512,128]{2,1,0:T(8,128)(2,1)S(1)}, bf16[6,512,128]{2,1,0:T(8,128)(2,1)}, u32[]{:S(2)}, u32[]{:S(2)}) collective-permute-start(bf16[6,512,128]{2,1,0:T(8,128)(2,1)S(1)} %collective-permute-done), channel_id=1, source_target_pairs={{0,28},{4,0},{8,4},{12,8},{16,12},{20,16},{24,20},{28,24},{1,29},{... | collective-permute-start | bytes 2359304 | tf_op jit(solution)/shard_map/ppermute | solution.py:57
  78.7 19.2 %collective-permute-start.5 = (bf16[6,512,128]{2,1,0:T(8,128)(2,1)S(1)}, bf16[6,512,128]{2,1,0:T(8,128)(2,1)S(1)}, u32[]{:S(2)}, u32[]{:S(2)}) collective-permute-start(bf16[6,512,128]{2,1,0:T(8,128)(2,1)S(1)} %collective-permute-done.3), channel_id=1, source_target_pairs={{0,4},{4,8},{8,12},{12,16},{16,20},{20,24},{24,28},{28,0},{1,5},{5... | collective-permute-start | bytes 2359304 | tf_op jit(solution)/shard_map/ppermute | solution.py:55
  80.3 23.1 %collective-permute-start.4 = (bf16[6,512,128]{2,1,0:T(8,128)(2,1)}, bf16[6,512,128]{2,1,0:T(8,128)(2,1)S(1)}, u32[]{:S(2)}, u32[]{:S(2)}) collective-permute-start(bf16[6,512,128]{2,1,0:T(8,128)(2,1)} %collective-permute-done.2), channel_id=1, source_target_pairs={{0,28},{4,0},{8,4},{12,8},{16,12},{20,16},{24,20},{28,24},{1,29},{... | collective-permute-start | bytes 2359304 | tf_op jit(solution)/shard_map/ppermute | solution.py:57
  97.9 12.4 %collective-permute-start.6 = (bf16[6,512,128]{2,1,0:T(8,128)(2,1)S(1)}, bf16[6,512,128]{2,1,0:T(8,128)(2,1)}, u32[]{:S(2)}, u32[]{:S(2)}) collective-permute-start(bf16[6,512,128]{2,1,0:T(8,128)(2,1)S(1)} %collective-permute-done.5), channel_id=1, source_target_pairs={{0,4},{4,8},{8,12},{12,16},{16,20},{20,24},{24,28},{28,0},{1,5},{5... | collective-permute-start | bytes 2359304 | tf_op jit(solution)/shard_map/ppermute | solution.py:55
  100.7 9.7 %copy-start = (f32[512,128,10]{1,2,0:T(8,128)S(1)}, f32[512,128,10]{1,2,0:T(8,128)}, u32[]{:S(2)}) copy-start(f32[512,128,10]{1,2,0:T(8,128)} %fusion.15) | copy-start | bytes 7864324
  123.7 191.3 %reduce-scatter.2.cloned.1.call-start = ((), (), s32[]{:S(2)}) async-start(), calls=%async_computation.2 | async-start | bytes 10616832 | tf_op jit(solution)/shard_map/reduce_scatter | solution.py:78
Sparse Core Ops, SparseCore 0:
  123.8 97.3 all-gather.2
  239.8 75.1 reduce-scatter.1
